TPU v7x, 32 devices: a whole 2x2x4 slice. The times are simulated.
32 devices in a mesh: kgrp: 4 (over x, core), tile: 8 (over z, y).
Axes of the slice: x: 2, y: 2, z: 4, core: 2. Of those that a mesh axis runs over, the one named last changes fastest.
Arguments:
- mask_spectrum: float32 [32, 2, 512, 512], P(('kgrp', 'tile')), may hold values from -6 to 6
- kernels: float32 [8, 2, 512, 512], P('kgrp', None, 'tile'), may hold values from -6 to 6
- owner_table: int32 [4], replicated, may hold values from 0 to 7
- step_weight: float32 [4], replicated, may hold values from 0.25 to 1
Outputs:
- intensity: float32 [32, 512, 512], P(('kgrp', 'tile'))
Inputs may be any that keep to these rules, and one draw needn't show every extreme that they name: `owner_table`: kernel indices, possibly repeated across steps.
All inputs are finite; a program needn't handle non-finite values.
Results may differ from a plain program's by a relative error of at most 0.0001.
Values sent between devices are 32-bit elements; how exact they have to be, the bound alone decides.
A program may use at most 128 MiB of HBM per device.

v0:
```python
import functools
import math

import jax
import jax.numpy as jnp
import ml_dtypes
import numpy as np
from jax import lax
from jax.experimental import pallas as pl
from jax.experimental.pallas import tpu as pltpu
from jax.sharding import PartitionSpec as P

MESH = pl.DeviceIdType.MESH
BF = jnp.bfloat16
F32 = jnp.float32


def split_np(x):
    hi = x.astype(np.float32).astype(ml_dtypes.bfloat16)
    lo = (x - hi.astype(np.float64)).astype(np.float32).astype(ml_dtypes.bfloat16)
    return hi, lo


def tables(n, radix):
    m = n // radix
    a = np.arange(m)
    rows = []
    for r in range(radix):
        phase = (a[:, None] * (r + radix * a[None, :])) % n * (2.0 * math.pi / n)
        c, s = np.cos(phase) / math.sqrt(n), np.sin(phase) / math.sqrt(n)
        rows.append(np.block([[c, s], [-s, c]]))
    b = np.stack(rows)
    bh, bl = split_np(b)
    row = np.concatenate([bh, bl], axis=1)
    col = np.concatenate([bh.transpose(0, 2, 1), bl.transpose(0, 2, 1)], axis=2)
    return row, col


def split(x):
    hi = x.astype(BF)
    return hi, (x - hi.astype(F32)).astype(BF)


def radix4(re, im):
    ar, ai, br, bi = re[0] + re[2], im[0] + im[2], re[0] - re[2], im[0] - im[2]
    cr, ci, dr, di = re[1] + re[3], im[1] + im[3], re[1] - re[3], im[1] - im[3]
    return [(ar + cr, ai + ci), (br - di, bi + dr), (ar - cr, ai - ci), (br + di, bi - dr)]


def kernel(dims, owner_ref, weight_ref, mask_hbm, kern_hbm, rowt_hbm, colt_hbm, out_ref,
           held, cand, mask, rowt, colt, lane_perm, stage, field, cols, total, blocks,
           z_send, z_recv, x_send, x_recv, y_send, y_recv, d_send, d_recv,
           c_send, c_recv, k_send, k_recv, loc):
    steps, groups, nk, nz, rows, n, m = dims
    g = lax.axis_index("kgrp")
    t = lax.axis_index("tile")
    x, c = g // 2, g % 2
    xo, co = 1 - x, 1 - c
    z, y = t // 2, t % 2
    yo = 1 - y
    x_peer, c_peer = {"kgrp": 2 * xo + c}, {"kgrp": 2 * x + co}
    y_peer = {"tile": 2 * z + yo}
    d_peer = {"kgrp": 2 * (x * (1 - c) + xo * c) + c, "tile": 2 * z + yo * (1 - c) + y * c}
    d_q = 2 * (xo * (1 - c) + x * c) + c
    d_y = y * (1 - c) + yo * c

    loads = [
        pltpu.make_async_copy(kern_hbm.at[:, :, :, pl.ds(pl.multiple_of(g * m, m), m)], cand.at[pl.ds(g * nk, nk)], loc.at[0]),
        pltpu.make_async_copy(mask_hbm, mask, loc.at[1]),
        pltpu.make_async_copy(rowt_hbm, rowt, loc.at[2]),
        pltpu.make_async_copy(colt_hbm, colt, loc.at[3]),
    ]
    for load in loads:
        load.start()

    barrier = pltpu.get_barrier_semaphore()
    for d in range(1, groups):
        pl.semaphore_signal(barrier, inc=1, device_id={"kgrp": (g + d) % groups}, device_id_type=MESH)
    pl.semaphore_signal(barrier, inc=1, device_id=y_peer, device_id_type=MESH)
    for d in range(1, nz):
        pl.semaphore_signal(barrier, inc=1, device_id={"tile": 2 * ((z + d) % nz) + y}, device_id_type=MESH)
    pl.semaphore_wait(barrier, groups + nz - 1)

    sent = []

    def send(src, dst, send_sem, recv_sem, device):
        copy = pltpu.make_async_remote_copy(src_ref=src, dst_ref=dst, send_sem=send_sem, recv_sem=recv_sem,
                                            device_id=device, device_id_type=MESH)
        copy.start()
        sent.append(copy)

    def arrive(ref, recv_sem):
        pltpu.make_async_remote_copy(src_ref=ref, dst_ref=ref, send_sem=recv_sem, recv_sem=recv_sem,
                                     device_id=c_peer, device_id_type=MESH).wait_recv()

    for d in range(1, groups):
        peer = (g + d) % groups
        send(kern_hbm.at[:, :, :, pl.ds(pl.multiple_of(peer * m, m), m)], cand.at[pl.ds(g * nk, nk)],
             k_send.at[d - 1], k_recv.at[d - 1], {"kgrp": peer})

    src_lane = lax.broadcasted_iota(jnp.int32, (n, n), 0)
    dst_lane = lax.broadcasted_iota(jnp.int32, (n, n), 1)
    radix = n // m
    lane_perm[...] = jnp.where((src_lane % m) * radix + src_lane // m == dst_lane, 1.0, 0.0).astype(BF)

    loads[0].wait()
    for d in range(1, groups):
        arrive(cand.at[pl.ds(((g + groups - d) % groups) * nk, nk)], k_recv.at[d - 1])
    for s in range(steps):
        held[s, g, :, z, y] = cand[owner_ref[s]]

    def near(d):
        return (z + d) % nz

    def piece(s, q, zz, yy):
        return held.at[s, q, :, zz, yy]

    def line(s, q, yy):
        return held.at[s, q, :, :, yy]

    def cross(s, d):
        own = piece(s, g, near(d), y)
        send(own, own, x_send.at[s, d], x_recv.at[s, d], x_peer)
        send(own, own, y_send.at[s, d], y_recv.at[s, d], y_peer)

    def to_core(s, kind, q, yy):
        send(line(s, q, yy), line(s, q, yy), c_send.at[s, kind], c_recv.at[s, kind], c_peer)

    def gather_z(s):
        for d in range(1, nz):
            arrive(piece(s, g, near(nz - d), y), z_recv.at[s, d])
            cross(s, nz - d)
        to_core(s, 0, g, y)

    def gather_xy(s):
        for d in [0] + [nz - d for d in range(1, nz)]:
            arrive(piece(s, 2 * xo + c, near(d), y), x_recv.at[s, d])
            arrive(piece(s, g, near(d), yo), y_recv.at[s, d])
            turned = piece(s, d_q, near(d), d_y)
            send(turned, turned, d_send.at[s, d], d_recv.at[s, d], d_peer)
        to_core(s, 1, 2 * xo + c, y)
        to_core(s, 2, g, yo)

    def gather_turned(s):
        for d in range(nz):
            arrive(piece(s, 2 * xo + c, near(d), yo), d_recv.at[s, d])
        to_core(s, 3, 2 * xo + c, yo)

    def rows_in(s, yy):
        for kind in (0, 1) if yy is y else (2, 3):
            arrive(line(s, 2 * x + co if kind % 2 == 0 else 2 * xo + co, yy), c_recv.at[s, kind])

        @pl.loop(0, nz)
        def _(zi):
            i = 2 * zi + yy
            at = pl.ds(pl.multiple_of(i * rows, rows), rows)
            re, im = [], []
            for q in range(groups):
                kr, ki = held[s, q, 0, zi, yy], held[s, q, 1, zi, yy]
                mr, mi = mask[0, at, q * m:(q + 1) * m], mask[1, at, q * m:(q + 1) * m]
                re.append(mr * kr - mi * ki)
                im.append(mr * ki + mi * kr)
            for r, (pr, pi) in enumerate(radix4(re, im)):
                for p, part in enumerate((pr, pi)):
                    hi, lo = split(part)
                    stage[r, at, p * m:(p + 1) * m] = hi
                    stage[r, at, (2 + p) * m:(3 + p) * m] = lo

    def compute(s):
        gather_turned(s)
        rows_in(s, y)
        rows_in(s, yo)
        for r in range(radix):
            hi, lo = stage[r, :, :2 * m], stage[r, :, 2 * m:]
            th, tl = rowt[r, :2 * m], rowt[r, 2 * m:]
            field[r] = jnp.dot(jnp.concatenate([hi, lo, hi], 1), jnp.concatenate([th, th, tl], 0),
                               preferred_element_type=F32)

        half = m // 4
        for ry in range(radix):
            @pl.loop(0, 4)
            def _(i):
                base = pl.multiple_of(i * half, half)
                re = [field[ry, pl.ds(k * m + base, half), :m] for k in range(radix)]
                im = [field[ry, pl.ds(k * m + base, half), m:] for k in range(radix)]
                for rx, parts in enumerate(radix4(re, im)):
                    for p, part in enumerate(parts):
                        hi, lo = split(part)
                        cols[rx, pl.ds(p * m + base, half), ry * m:(ry + 1) * m] = hi
                        cols[rx, pl.ds((2 + p) * m + base, half), ry * m:(ry + 1) * m] = lo

        for rx in range(radix):
            hi, lo = cols[rx, :2 * m], cols[rx, 2 * m:]
            th, tl = colt[rx, :, :2 * m], colt[rx, :, 2 * m:]
            done = jnp.dot(jnp.concatenate([th, th, tl], 1), jnp.concatenate([hi, lo, hi], 0),
                           preferred_element_type=F32)
            power = (done[:m] * done[:m] + done[m:] * done[m:]) * weight_ref[s]
            if s == 0:
                total[rx] = power
            else:
                total[rx] += power

    for s in range(steps):
        own = piece(s, g, z, y)
        for d in range(1, nz):
            send(own, own, z_send.at[s, d], z_recv.at[s, d], {"tile": 2 * near(d) + y})
        cross(s, 0)
    for load in loads[1:]:
        load.wait()
    gather_z(0)
    for s in range(steps):
        if s + 1 < steps:
            gather_z(s + 1)
        gather_xy(s)
        if s:
            compute(s - 1)
    compute(steps - 1)

    for rx in range(radix):
        hi, lo = split(total[rx])
        perm = lane_perm[...]
        image = jnp.dot(jnp.concatenate([hi, lo], 1), jnp.concatenate([perm, perm], 0), preferred_element_type=F32)
        for q in range(radix):
            blocks[q, pl.ds(rx, m, stride=radix), :] = image[:, q * m:(q + 1) * m]
    for q in range(radix):
        out_ref[:, q * m:(q + 1) * m] = blocks[q]
    for copy in sent:
        copy.wait_send()


def local(mesh_shape, mask_spectrum, kernels, owner_table, step_weight):
    groups, tiles = mesh_shape
    nk, _, rows, n = kernels.shape
    steps = owner_table.shape[0]
    m = n // groups
    radix = groups
    nz = tiles // 2
    rowt, colt = tables(n, radix)
    dma = pltpu.SemaphoreType.DMA
    any_spec = pl.BlockSpec(memory_space=pl.ANY)
    smem = pl.BlockSpec(memory_space=pltpu.SMEM)
    out = pl.pallas_call(
        functools.partial(kernel, (steps, groups, nk, nz, rows, n, m)),
        out_shape=jax.ShapeDtypeStruct((n, n), F32),
        in_specs=[smem, smem, any_spec, any_spec, any_spec, any_spec],
        out_specs=pl.BlockSpec(memory_space=pltpu.VMEM),
        scratch_shapes=[
            pltpu.VMEM((steps, groups, 2, nz, 2, rows, m), F32),
            pltpu.VMEM((groups * nk, 2, rows, m), F32),
            pltpu.VMEM((2, n, n), F32),
            pltpu.VMEM(rowt.shape, BF),
            pltpu.VMEM(colt.shape, BF),
            pltpu.VMEM((n, n), BF),
            pltpu.VMEM((radix, n, 4 * m), BF),
            pltpu.VMEM((radix, n, 2 * m), F32),
            pltpu.VMEM((radix, 4 * m, n), BF),
            pltpu.VMEM((radix, m, n), F32),
            pltpu.VMEM((radix, n, m), F32),
        ] + [dma((steps, nz))] * 8 + [dma((steps, 4))] * 2 + [dma((groups - 1,))] * 2 + [dma((4,))],
        compiler_params=pltpu.CompilerParams(collective_id=0, has_side_effects=True, vmem_limit_bytes=62 * 1024 * 1024),
    )(owner_table, step_weight, mask_spectrum[0], kernels, jnp.asarray(rowt), jnp.asarray(colt))
    return out[None]


def solution(mesh):
    in_specs = (P(("kgrp", "tile"), None, None, None), P("kgrp", None, "tile", None), P(), P())
    out_specs = P(("kgrp", "tile"), None, None)
    body = functools.partial(local, (mesh.shape["kgrp"], mesh.shape["tile"]))
    return jax.shard_map(body, mesh=mesh, in_specs=in_specs, out_specs=out_specs, check_vma=False)
```

profile of v0, /device:TPU:0, one launch (start us, length us, event | category | flops | bytes accessed | tf_op | source)
XLA Modules:
  0.0 64.2 jit_solution(9317424262586710436)
XLA Ops:
  0.0 62.0 %shard_map.64 = f32[512,512]{1,0:T(8,128)} custom-call(s32[4]{0:T(128)} %owner_ref.1, f32[4]{0:T(128)} %weight_ref.1, f32[2,512,512]{2,1,0:T(8,128)} %bitcast.3, f32[2,2,64,512]{3,2,1,0:T(8,128)} %kern_hbm.1, bf16[4,512,256]{2,1,0:T(8,128)(2,1)} %constant.4.clone.rowt_hbm, bf16[4,256,512]{2,1,0:T(8,128)(2,1)} %constant.5.clone.colt_hbm), custom_call_target="tpu_custom_call" | custom-call | tf_op jit(solution)/shard_map/pallas_call | solution.py:242
  62.0 2.3 %copy.8 = f32[1,512,512]{2,1,0:T(8,128)} copy(f32[1,512,512]{2,1,0:T(8,128)} %bitcast.2) | data formatting | bytes 2097152
where the time goes:
time: 64.4 us; the launch traced here: 64.2 us
  Pallas kernels  62 us (96%)
  local copies, waits for them, and re-layouts  2.26 us (4%)
    pallas_call x1, Pallas kernels, local(): pl.pallas_call(functools.partial(kernel, (steps, groups, nk, nz, rows, n,...  62 us
    unnamed x1, local copies, waits for them, and re-layouts  2.26 us

commit v1 on v0

v1 whole, which is shorter than its diff:
```python
import functools
import math

import jax
import jax.numpy as jnp
import ml_dtypes
import numpy as np
from jax import lax
from jax.experimental import pallas as pl
from jax.experimental.pallas import tpu as pltpu
from jax.sharding import PartitionSpec as P

MESH = pl.DeviceIdType.MESH
BF = jnp.bfloat16
F32 = jnp.float32


def split_np(x):
    hi = x.astype(np.float32).astype(ml_dtypes.bfloat16)
    lo = (x - hi.astype(np.float64)).astype(np.float32).astype(ml_dtypes.bfloat16)
    return hi, lo


def tables(n, radix):
    m = n // radix
    a = np.arange(m)
    rows = []
    for r in range(radix):
        phase = (a[:, None] * (r + radix * a[None, :])) % n * (2.0 * math.pi / n)
        c, s = np.cos(phase) / math.sqrt(n), np.sin(phase) / math.sqrt(n)
        rows.append(np.block([[c, s], [-s, c]]))
    b = np.stack(rows)
    bh, bl = split_np(b)
    row = np.concatenate([bh, bl], axis=1)
    col = np.concatenate([bh.transpose(0, 2, 1), bl.transpose(0, 2, 1)], axis=2)
    return row, col


def split(x):
    hi = x.astype(BF)
    return hi, (x - hi.astype(F32)).astype(BF)


def radix4(re, im):
    ar, ai, br, bi = re[0] + re[2], im[0] + im[2], re[0] - re[2], im[0] - im[2]
    cr, ci, dr, di = re[1] + re[3], im[1] + im[3], re[1] - re[3], im[1] - im[3]
    return [(ar + cr, ai + ci), (br - di, bi + dr), (ar - cr, ai - ci), (br + di, bi - dr)]


OWN, Z_IN, Y_IN, ACROSS, ROWS, COLUMNS = range(6)
TUNED = {
    (2, 4, 4, 3, 4): [
        (0, 0, 0), (0, 0, 1), (0, 0, 2), (1, 0, 1, 0), (0, 1, 0), (1, 0, 1, 1), (1, 0, 2, 0), (0, 0, 3),
        (2, 0, 1, 0), (1, 0, 1, 2), (1, 0, 2, 1), (1, 0, 3, 0), (1, 0, 2, 2), (0, 1, 1), (4, 0, 2, 0), (2, 0, 0, 0),
        (4, 0, 1, 0), (4, 0, 0, 0), (1, 1, 1, 0), (2, 0, 2, 0), (2, 0, 0, 1), (2, 1, 0, 0), (1, 0, 3, 1), (0, 1, 2),
        (1, 0, 3, 2), (1, 1, 1, 1), (2, 0, 1, 1), (4, 0, 3, 0), (2, 0, 3, 0), (2, 0, 0, 2), (4, 0, 0, 1), (2, 0, 3, 1),
        (1, 1, 2, 0), (1, 1, 1, 2), (0, 1, 3), (2, 0, 2, 1), (2, 0, 1, 2), (3, 1, 0), (4, 1, 0, 0), (1, 1, 3, 0),
        (2, 0, 2, 2), (4, 1, 1, 0), (4, 0, 2, 1), (2, 0, 3, 2), (4, 0, 3, 1), (1, 1, 2, 1), (2, 1, 0, 1), (1, 1, 2, 2),
        (3, 1, 1), (2, 1, 0, 2), (4, 0, 1, 1), (3, 1, 2), (2, 1, 1, 0), (4, 1, 2, 0), (5, 0, 1, 0), (2, 1, 2, 0),
        (5, 0, 1, 1), (1, 1, 3, 1), (4, 1, 0, 1), (5, 0, 1, 2), (5, 0, 1, 3), (2, 1, 2, 1), (2, 1, 3, 0), (1, 1, 3, 2),
        (5, 0, 0, 0), (5, 0, 0, 1), (2, 1, 1, 1), (5, 0, 0, 2), (4, 1, 3, 0), (2, 1, 3, 1), (2, 1, 2, 2), (5, 0, 0, 3),
        (2, 1, 1, 2), (4, 1, 1, 1), (4, 1, 2, 1), (2, 1, 3, 2), (4, 1, 3, 1), (5, 1, 1, 0), (5, 1, 1, 1), (5, 1, 1, 2),
        (5, 1, 1, 3), (5, 1, 0, 0), (5, 1, 0, 1), (5, 1, 0, 2), (5, 1, 0, 3),
    ],
}


def program(spc, nz, pieces, parts, radix):
    key = (spc, nz, pieces, len(parts), radix)
    if key in TUNED:
        return TUNED[key]
    order = []
    for l in range(spc):
        order += [(OWN, l, p) for p in range(pieces)]
        end = l == spc - 1
        for j in range(nz):
            order += [(Z_IN, l, j, p) for p in parts if j]
            order += [(Y_IN, l, j, p) for p in parts if not (end and j == 1)]
        order += [(ACROSS, l, p) for p in parts if end]
        order += [(Y_IN, l, 1, p) for p in parts if end]
        order += [(ROWS, l, k, other) for k in range(nz) for other in (0, 1)]
        order += [(COLUMNS, l, tile, rx) for tile in (1, 0) for rx in range(radix)]
    return order


def kernel(dims, owner_ref, weight_ref, mask_hbm, kern_hbm, rowt_hbm, colt_hbm, out_ref,
           kern, side, held, mask, rowt, colt, lane_perm, stage, field, cols, total, part, blocks,
           loc, k_send, k_recv, m_send, m_recv, e_send, e_recv, up_send, down_send, relay_send, z_recv,
           y_send, y_recv, across_up, across_down, x_send, x_recv, p_send, p_recv):
    spc, nk, nz, rows, n, radix = dims
    m = n // radix
    last = spc - 1
    g = lax.axis_index("kgrp")
    t = lax.axis_index("tile")
    x, c = g // 2, g % 2
    z, y = t // 2, t % 2
    xo, co, yo = 1 - x, 1 - c, 1 - y
    x_peer, c_peer = {"kgrp": 2 * xo + c}, {"kgrp": 2 * x + co}
    y_peer = {"tile": 2 * z + yo}

    def at_z(i):
        return {"tile": 2 * i + y}

    unit = 8
    nt = rows // unit
    share = nt // 4
    keep = nt - share
    wide = max(share, 1)
    cuts = [(i, i + wide) for i in range(0, nt, wide)]
    parts = [p for p, cut in enumerate(cuts) if cut[1] <= keep]

    def span(s, p):
        a, b = cuts[p]
        return pl.ds(pl.multiple_of(a * unit + s * (rows - unit * (a + b)), unit), unit * (b - a))

    own_kern = kern.at[pl.ds(c * nk, nk)]
    loads = [
        pltpu.make_async_copy(kern_hbm, own_kern, loc.at[0]),
        pltpu.make_async_copy(mask_hbm, mask.at[0], loc.at[1]),
        pltpu.make_async_copy(rowt_hbm, rowt, loc.at[2]),
        pltpu.make_async_copy(colt_hbm, colt, loc.at[3]),
    ]
    for load in loads:
        load.start()

    barrier = pltpu.get_barrier_semaphore()
    for peer in (c_peer, x_peer, y_peer):
        pl.semaphore_signal(barrier, inc=1, device_id=peer, device_id_type=MESH)

    @pl.when(z > 0)
    def _():
        pl.semaphore_signal(barrier, inc=1, device_id=at_z(z - 1), device_id_type=MESH)

    @pl.when(z < nz - 1)
    def _():
        pl.semaphore_signal(barrier, inc=1, device_id=at_z(z + 1), device_id_type=MESH)

    src_lane = lax.broadcasted_iota(jnp.int32, (n, n), 0)
    dst_lane = lax.broadcasted_iota(jnp.int32, (n, n), 1)
    lane_perm[...] = jnp.where((src_lane % m) * radix + src_lane // m == dst_lane, 1.0, 0.0).astype(BF)
    loads[0].wait()

    pl.semaphore_wait(barrier, 3 + jnp.minimum(z, 1) + jnp.minimum(nz - 1 - z, 1))

    sent = []

    def send(src, dst, send_sem, recv_sem, device, cond=None):
        copy = pltpu.make_async_remote_copy(src_ref=src, dst_ref=dst, send_sem=send_sem, recv_sem=recv_sem,
                                            device_id=device, device_id_type=MESH)
        if cond is None:
            copy.start()
        else:
            pl.when(cond)(copy.start)
        sent.append((copy, cond))

    def arrive(ref, recv_sem):
        pltpu.make_async_remote_copy(src_ref=ref, dst_ref=ref, send_sem=recv_sem, recv_sem=recv_sem,
                                     device_id=c_peer, device_id_type=MESH).wait_recv()

    def piece(l, zz, yy, s, p):
        return held.at[l, zz, yy, :, span(s, p)]

    for p in range(len(cuts)):
        src = kern.at[pl.ds(c * nk, nk), :, span(xo, p)]
        send(src, src, k_send.at[p], k_recv.at[p], c_peer)
    send(mask_hbm, mask.at[1], m_send.at[0], m_recv.at[0], c_peer)

    owners = [owner_ref[c * spc + l] for l in range(spc)]
    for p in range(len(cuts)):
        arrive(kern.at[pl.ds(co * nk, nk), :, span(xo, p)], k_recv.at[p])
    for l in range(spc):
        for p in range(len(cuts)):
            side[x, l, :, span(xo, p)] = kern[owners[l] % (2 * nk), :, span(xo, p)]
    for l in range(spc):
        for p in range(len(cuts)):
            src = side.at[x, l, :, span(xo, p)]
            send(src, src, e_send.at[l, p], e_recv.at[l, p], x_peer)

    def own(l, p):
        arrive(side.at[xo, l, :, span(x, p)], e_recv.at[l, p])
        mine = owners[l] // (2 * nk) == x
        held[l, z, y, :, span(x, p)] = jnp.where(mine, side[x, l, :, span(x, p)], side[xo, l, :, span(x, p)])
        if p in parts:
            here = piece(l, z, y, x, p)
            send(here, here, y_send.at[l, z, p], y_recv.at[l, z, p], y_peer)
            send(here, here, down_send.at[l, p], z_recv.at[l, z, p], at_z(z - 1), z > 0)
            send(here, here, up_send.at[l, p], z_recv.at[l, z, p], at_z(z + 1), z < nz - 1)

    def across(l, p):
        here = piece(l, z, yo, x, p)
        send(here, here, across_down.at[p], y_recv.at[l, z, p], at_z(z - 1), z > 0)
        send(here, here, across_up.at[p], y_recv.at[l, z, p], at_z(z + 1), z < nz - 1)

    def share_x(l, zz, yy, cond=None):
        if share:
            here = piece(l, zz, yy, x, 0)
            send(here, here, x_send.at[l, zz, yy], x_recv.at[l, zz, yy], x_peer, cond)

    def z_in(l, j, p):
        for zz, have, dest, more in ((z + j, z + j < nz, z - 1, z > 0), (z - j, z >= j, z + 1, z < nz - 1)):
            here = piece(l, zz, y, x, p)
            pl.when(have)(functools.partial(arrive, here, z_recv.at[l, zz, p]))
            if j < nz - 1:
                send(here, here, relay_send.at[l, zz, p], z_recv.at[l, zz, p], at_z(dest), have & more)
            if l != last or j > 1:
                send(here, here, y_send.at[l, zz, p], y_recv.at[l, zz, p], y_peer, have)
            if p == 0:
                share_x(l, zz, y, have)

    def y_in(l, j, p):
        if j == 0:
            arrive(piece(l, z, yo, x, p), y_recv.at[l, z, p])
            if p == 0:
                share_x(l, z, yo)
            return
        for zz, have in ((z + j, z + j < nz), (z - j, z >= j)):
            pl.when(have)(functools.partial(arrive, piece(l, zz, yo, x, p), y_recv.at[l, zz, p]))
            if p == 0:
                share_x(l, zz, yo, have)

    def near(k):
        if k == 0:
            return z
        low = jnp.minimum(z, nz - 1 - z)
        both = z + (k + 1) // 2 if k % 2 else z - k // 2
        one = jnp.where(low == z, z + k - low, z - k + low)
        return jnp.where(k <= 2 * low, both, one)

    def x_in(l, k, yy):
        if share and not (k == 0 and yy is y):
            arrive(piece(l, near(k), yy, xo, 0), x_recv.at[l, near(k), yy])

    def rows_in(l, blocks_in):
        for j, (k, yy) in enumerate(blocks_in):
            zi = near(k)
            i = 2 * zi + yy
            at = pl.ds(pl.multiple_of(i * rows, rows), rows)

            @pl.loop(0, 2)
            def _(tile):
                to = pl.ds(pl.multiple_of((2 * j + tile) * rows, rows), rows)
                re, im = [], []
                for q in range(radix):
                    kr, ki = held[l, zi, yy, 0, :, q * m:(q + 1) * m], held[l, zi, yy, 1, :, q * m:(q + 1) * m]
                    mr, mi = mask[tile, 0, at, q * m:(q + 1) * m], mask[tile, 1, at, q * m:(q + 1) * m]
                    re.append(mr * kr - mi * ki)
                    im.append(mr * ki + mi * kr)
                for r, (pr, pi) in enumerate(radix4(re, im)):
                    for p, v in enumerate((pr, pi)):
                        hi, lo = split(v)
                        stage[r, to, p * m:(p + 1) * m] = hi
                        stage[r, to, (2 + p) * m:(3 + p) * m] = lo

        size = 2 * len(blocks_in) * rows
        for r in range(radix):
            hi, lo = stage[r, :size, :2 * m], stage[r, :size, 2 * m:]
            th, tl = rowt[r, :2 * m], rowt[r, 2 * m:]
            done = jnp.dot(jnp.concatenate([hi, lo, hi], 1), jnp.concatenate([th, th, tl], 0),
                           preferred_element_type=F32)
            for j, (k, yy) in enumerate(blocks_in):
                i = 2 * near(k) + yy
                for tile in range(2):
                    field[l, r, tile, pl.ds(pl.multiple_of(i * rows, rows), rows)] = (
                        done[(2 * j + tile) * rows:(2 * j + tile + 1) * rows])

    half = m // 4

    def middle(l, tile):
        for ry in range(radix):
            @pl.loop(0, 4)
            def _(i):
                base = pl.multiple_of(i * half, half)
                re = [field[l, ry, tile, pl.ds(k * m + base, half), :m] for k in range(radix)]
                im = [field[l, ry, tile, pl.ds(k * m + base, half), m:] for k in range(radix)]
                for rx, pair in enumerate(radix4(re, im)):
                    for p, v in enumerate(pair):
                        hi, lo = split(v)
                        cols[rx, pl.ds(p * m + base, half), ry * m:(ry + 1) * m] = hi
                        cols[rx, pl.ds((2 + p) * m + base, half), ry * m:(ry + 1) * m] = lo

    def columns(l, tile, rx):
        hi, lo = cols[rx, :2 * m], cols[rx, 2 * m:]
        th, tl = colt[rx, :, :2 * m], colt[rx, :, 2 * m:]
        done = jnp.dot(jnp.concatenate([th, th, tl], 1), jnp.concatenate([hi, lo, hi], 0),
                       preferred_element_type=F32)
        power = (done[:m] * done[:m] + done[m:] * done[m:]) * weight_ref[c * spc + l]
        if l == 0:
            total[tile, rx] = power
        else:
            total[tile, rx] += power

    def row_step(l, k, other):
        yy = yo if other else y
        x_in(l, k, yy)
        rows_in(l, [(k, yy)])

    def column_step(l, tile, rx):
        if rx == 0:
            middle(l, tile)
        columns(l, tile, rx)
        if l == last and tile == 1:
            for done in [rx - 1] if rx < radix - 1 else [rx - 1, rx]:
                if done >= 0:
                    send(total.at[1, done], part.at[done], p_send.at[done], p_recv.at[done], c_peer)

    steps = (own, z_in, y_in, across, row_step, column_step)
    first_row = True
    for op, *args in program(spc, nz, len(cuts), parts, radix):
        if op == 4 and first_row:
            first_row = False
            for load in loads[1:]:
                load.wait()
            arrive(mask.at[1], m_recv.at[0])
        steps[op](*args)

    for rx in range(radix):
        arrive(part.at[rx], p_recv.at[rx])
        hi, lo = split(total[0, rx] + part[rx])
        perm = lane_perm[...]
        image = jnp.dot(jnp.concatenate([hi, lo], 1), jnp.concatenate([perm, perm], 0), preferred_element_type=F32)
        for q in range(radix):
            blocks[q, pl.ds(rx, m, stride=radix), :] = image[:, q * m:(q + 1) * m]
    for q in range(radix):
        out_ref[:, q * m:(q + 1) * m] = blocks[q]
    for copy, cond in sent:
        if cond is None:
            copy.wait_send()
        else:
            pl.when(cond)(copy.wait_send)


def local(mesh_shape, mask_spectrum, kernels, owner_table, step_weight):
    groups, tiles = mesh_shape
    nk, _, rows, n = kernels.shape
    steps = owner_table.shape[0]
    radix = 4
    m = n // radix
    spc = steps // 2
    nz = tiles // 2
    most = rows // 8
    rowt, colt = tables(n, radix)
    dma = pltpu.SemaphoreType.DMA
    any_spec = pl.BlockSpec(memory_space=pl.ANY)
    smem = pl.BlockSpec(memory_space=pltpu.SMEM)
    out = pl.pallas_call(
        functools.partial(kernel, (spc, nk, nz, rows, n, radix)),
        out_shape=jax.ShapeDtypeStruct((n, n), F32),
        in_specs=[smem, smem, any_spec, any_spec, any_spec, any_spec],
        out_specs=pl.BlockSpec(memory_space=pltpu.VMEM),
        scratch_shapes=[
            pltpu.VMEM((2 * nk, 2, rows, n), F32),
            pltpu.VMEM((2, spc, 2, rows, n), F32),
            pltpu.VMEM((spc, nz, 2, 2, rows, n), F32),
            pltpu.VMEM((2, 2, n, n), F32),
            pltpu.VMEM(rowt.shape, BF),
            pltpu.VMEM(colt.shape, BF),
            pltpu.VMEM((n, n), BF),
            pltpu.VMEM((radix, 4 * rows, 4 * m), BF),
            pltpu.VMEM((spc, radix, 2, n, 2 * m), F32),
            pltpu.VMEM((radix, 4 * m, n), BF),
            pltpu.VMEM((2, radix, m, n), F32),
            pltpu.VMEM((radix, m, n), F32),
            pltpu.VMEM((radix, n, m), F32),
            dma((4,)), dma((most,)), dma((most,)), dma((1,)), dma((1,)), dma((spc, most)), dma((spc, most)),
            dma((spc, most)), dma((spc, most)), dma((spc, nz, most)), dma((spc, nz, most)),
            dma((spc, nz, most)), dma((spc, nz, most)), dma((most,)), dma((most,)),
            dma((spc, nz, 2)), dma((spc, nz, 2)), dma((radix,)), dma((radix,)),
        ],
        compiler_params=pltpu.CompilerParams(collective_id=0, has_side_effects=True, vmem_limit_bytes=54 * 1024 * 1024),
    )(owner_table, step_weight, mask_spectrum[0], kernels, jnp.asarray(rowt), jnp.asarray(colt))
    return out[None]


def solution(mesh):
    in_specs = (P(("kgrp", "tile"), None, None, None), P("kgrp", None, "tile", None), P(), P())
    out_specs = P(("kgrp", "tile"), None, None)
    body = functools.partial(local, (mesh.shape["kgrp"], mesh.shape["tile"]))
    return jax.shard_map(body, mesh=mesh, in_specs=in_specs, out_specs=out_specs, check_vma=False)
```

time: 64.4 us -> 56.5 us (0.88)
  Pallas kernels: 62 us -> 54.1 us
    pallas_call x1, Pallas kernels: 62 us -> 54.1 us  [local(): pl.pallas_call(functools.partial(kernel, (spc, nk, nz, rows, n, radix)),...]
where the time goes in v1:
time: 56.5 us; the launch traced here: 56.4 us
  Pallas kernels  54.1 us (96%)
  local copies, waits for them, and re-layouts  2.26 us (4%)
    pallas_call x1, Pallas kernels, local(): pl.pallas_call(functools.partial(kernel, (spc, nk, nz, rows, n, radix)),...  54.1 us
    unnamed x1, local copies, waits for them, and re-layouts  2.26 us

profile of v1, /device:TPU:0, one launch (start us, length us, event | category | flops | bytes accessed | tf_op | source)
XLA Modules:
  0.0 56.4 jit_solution(11202058776265409761)
XLA Ops:
  0.0 54.1 %shard_map.64 = f32[512,512]{1,0:T(8,128)} custom-call(s32[4]{0:T(128)} %owner_ref.1, f32[4]{0:T(128)} %weight_ref.1, f32[2,512,512]{2,1,0:T(8,128)} %bitcast.3, f32[2,2,64,512]{3,2,1,0:T(8,128)} %kern_hbm.1, bf16[4,512,256]{2,1,0:T(8,128)(2,1)} %constant.4.clone.rowt_hbm, bf16[4,256,512]{2,1,0:T(8,128)(2,1)} %constant.5.clone.colt_hbm), custom_call_target="tpu_custom_call" | custom-call | tf_op jit(solution)/shard_map/pallas_call | solution.py:345
  54.1 2.3 %copy.8 = f32[1,512,512]{2,1,0:T(8,128)} copy(f32[1,512,512]{2,1,0:T(8,128)} %bitcast.2) | data formatting | bytes 2097152

commit v2 on v1

v2 whole, which is shorter than its diff:
```python
import functools
import math

import jax
import jax.numpy as jnp
import ml_dtypes
import numpy as np
from jax import lax
from jax.experimental import pallas as pl
from jax.experimental.pallas import tpu as pltpu
from jax.sharding import PartitionSpec as P

MESH = pl.DeviceIdType.MESH
BF = jnp.bfloat16
F32 = jnp.float32


def split_np(x):
    hi = x.astype(np.float32).astype(ml_dtypes.bfloat16)
    lo = (x - hi.astype(np.float64)).astype(np.float32).astype(ml_dtypes.bfloat16)
    return hi, lo


def tables(n, radix):
    m = n // radix
    a = np.arange(m)
    rows = []
    for r in range(radix):
        phase = (a[:, None] * (r + radix * a[None, :])) % n * (2.0 * math.pi / n)
        c, s = np.cos(phase) / math.sqrt(n), np.sin(phase) / math.sqrt(n)
        rows.append(np.block([[c, s], [-s, c]]))
    b = np.stack(rows)
    bh, bl = split_np(b)
    row = np.concatenate([bh, bl], axis=1)
    col = np.concatenate([bh.transpose(0, 2, 1), bl.transpose(0, 2, 1)], axis=2)
    return row, col


def split(x):
    hi = x.astype(BF)
    return hi, (x - hi.astype(F32)).astype(BF)


def radix4(re, im):
    ar, ai, br, bi = re[0] + re[2], im[0] + im[2], re[0] - re[2], im[0] - im[2]
    cr, ci, dr, di = re[1] + re[3], im[1] + im[3], re[1] - re[3], im[1] - im[3]
    return [(ar + cr, ai + ci), (br - di, bi + dr), (ar - cr, ai - ci), (br + di, bi - dr)]


OWN, Z_IN, Y_IN, ACROSS, ROWS, COLUMNS = range(6)
TUNED = {
    (2, 4, 4, 3, 4): [
        (0, 0, 0), (0, 0, 1), (0, 0, 2), (1, 0, 1, 0), (0, 1, 0), (1, 0, 1, 1), (1, 0, 2, 0), (0, 0, 3),
        (2, 0, 1, 0), (1, 0, 1, 2), (1, 0, 2, 1), (1, 0, 3, 0), (1, 0, 2, 2), (0, 1, 1), (4, 0, 2, 0), (2, 0, 0, 0),
        (4, 0, 1, 0), (4, 0, 0, 0), (1, 1, 1, 0), (2, 0, 2, 0), (2, 0, 0, 1), (2, 1, 0, 0), (1, 0, 3, 1), (0, 1, 2),
        (1, 0, 3, 2), (1, 1, 1, 1), (2, 0, 1, 1), (4, 0, 3, 0), (2, 0, 3, 0), (2, 0, 0, 2), (4, 0, 0, 1), (2, 0, 3, 1),
        (1, 1, 2, 0), (1, 1, 1, 2), (0, 1, 3), (2, 0, 2, 1), (2, 0, 1, 2), (3, 1, 0), (4, 1, 0, 0), (1, 1, 3, 0),
        (2, 0, 2, 2), (4, 1, 1, 0), (4, 0, 2, 1), (2, 0, 3, 2), (4, 0, 3, 1), (1, 1, 2, 1), (2, 1, 0, 1), (1, 1, 2, 2),
        (3, 1, 1), (2, 1, 0, 2), (4, 0, 1, 1), (3, 1, 2), (2, 1, 1, 0), (4, 1, 2, 0), (5, 0, 1, 0), (2, 1, 2, 0),
        (5, 0, 1, 1), (1, 1, 3, 1), (4, 1, 0, 1), (5, 0, 1, 2), (5, 0, 1, 3), (2, 1, 2, 1), (2, 1, 3, 0), (1, 1, 3, 2),
        (5, 0, 0, 0), (5, 0, 0, 1), (2, 1, 1, 1), (5, 0, 0, 2), (4, 1, 3, 0), (2, 1, 3, 1), (2, 1, 2, 2), (5, 0, 0, 3),
        (2, 1, 1, 2), (4, 1, 1, 1), (4, 1, 2, 1), (2, 1, 3, 2), (4, 1, 3, 1), (5, 1, 1, 0), (5, 1, 1, 1), (5, 1, 1, 2),
        (5, 1, 1, 3), (5, 1, 0, 0), (5, 1, 0, 1), (5, 1, 0, 2), (5, 1, 0, 3),
    ],
}


def program(spc, nz, pieces, parts, radix):
    key = (spc, nz, pieces, len(parts), radix)
    if key in TUNED:
        return TUNED[key]
    order = []
    for l in range(spc):
        order += [(OWN, l, p) for p in range(pieces)]
        end = l == spc - 1
        for j in range(nz):
            order += [(Z_IN, l, j, p) for p in parts if j]
            order += [(Y_IN, l, j, p) for p in parts if not (end and j == 1)]
        order += [(ACROSS, l, p) for p in parts if end]
        order += [(Y_IN, l, 1, p) for p in parts if end]
        order += [(ROWS, l, k, other) for k in range(nz) for other in (0, 1)]
        order += [(COLUMNS, l, tile, rx) for tile in (1, 0) for rx in range(radix)]
    return order


def kernel(dims, owner_ref, weight_ref, mask_hbm, kern_hbm, rowt_hbm, colt_hbm, out_ref,
           kern, side, held, mask, rowt, colt, lane_perm, stage, field, cols, total, part, blocks,
           loc, k_recv, m_recv, e_recv, z_recv, y_recv, x_recv, p_recv, gone):
    spc, nk, nz, rows, n, radix = dims
    m = n // radix
    last = spc - 1
    g = lax.axis_index("kgrp")
    t = lax.axis_index("tile")
    x, c = g // 2, g % 2
    z, y = t // 2, t % 2
    xo, co, yo = 1 - x, 1 - c, 1 - y
    x_peer, c_peer = {"kgrp": 2 * xo + c}, {"kgrp": 2 * x + co}
    y_peer = {"tile": 2 * z + yo}

    def at_z(i):
        return {"tile": 2 * i + y}

    unit = 8
    nt = rows // unit
    share = nt // 4
    keep = nt - share
    wide = max(share, 1)
    cuts = [(i, i + wide) for i in range(0, nt, wide)]
    parts = [p for p, cut in enumerate(cuts) if cut[1] <= keep]

    def span(s, p):
        a, b = cuts[p]
        return pl.ds(pl.multiple_of(a * unit + s * (rows - unit * (a + b)), unit), unit * (b - a))

    barrier = pltpu.get_barrier_semaphore()
    for peer in (c_peer, x_peer, y_peer):
        pl.semaphore_signal(barrier, inc=1, device_id=peer, device_id_type=MESH)

    @pl.when(z > 0)
    def _():
        pl.semaphore_signal(barrier, inc=1, device_id=at_z(z - 1), device_id_type=MESH)

    @pl.when(z < nz - 1)
    def _():
        pl.semaphore_signal(barrier, inc=1, device_id=at_z(z + 1), device_id_type=MESH)

    own_kern = kern.at[pl.ds(c * nk, nk)]
    loads = [
        pltpu.make_async_copy(kern_hbm, own_kern, loc.at[0]),
        pltpu.make_async_copy(mask_hbm, mask.at[0], loc.at[1]),
        pltpu.make_async_copy(rowt_hbm, rowt, loc.at[2]),
        pltpu.make_async_copy(colt_hbm, colt, loc.at[3]),
    ]
    for load in loads:
        load.start()
    loads[0].wait()
    pl.semaphore_wait(barrier, 3 + jnp.minimum(z, 1) + jnp.minimum(nz - 1 - z, 1))

    groups = {}

    def send(src, dst, recv_sem, device, group, cond=None):
        index, _, size = groups.setdefault(group, (len(groups), cond, 0))
        groups[group] = index, cond, size + math.prod(src.shape) // n
        copy = pltpu.make_async_remote_copy(src_ref=src, dst_ref=dst, send_sem=gone.at[index], recv_sem=recv_sem,
                                            device_id=device, device_id_type=MESH)
        if cond is None:
            copy.start()
        else:
            pl.when(cond)(copy.start)

    def all_gone():
        for index, cond, size in groups.values():
            if size <= n:
                ref = mask.at[0, 0, pl.ds(0, size)]
            elif size <= 2 * n:
                ref = mask.at[0, :, pl.ds(0, size // 2)]
            else:
                ref = mask.at[:, :, pl.ds(0, size // 4)]
            wait = pltpu.make_async_remote_copy(src_ref=ref, dst_ref=ref, send_sem=gone.at[index],
                                                recv_sem=gone.at[index], device_id=c_peer, device_id_type=MESH).wait_send
            if cond is None:
                wait()
            else:
                pl.when(cond)(wait)

    def arrive(ref, recv_sem):
        pltpu.make_async_remote_copy(src_ref=ref, dst_ref=ref, send_sem=recv_sem, recv_sem=recv_sem,
                                     device_id=c_peer, device_id_type=MESH).wait_recv()

    def piece(l, zz, yy, s, p):
        return held.at[l, zz, yy, :, span(s, p)]

    for p in range(len(cuts)):
        src = kern.at[pl.ds(c * nk, nk), :, span(xo, p)]
        send(src, src, k_recv.at[p], c_peer, "core")
    send(mask_hbm, mask.at[1], m_recv.at[0], c_peer, "mask")

    owners = [owner_ref[c * spc + l] for l in range(spc)]
    for p in range(len(cuts)):
        arrive(kern.at[pl.ds(co * nk, nk), :, span(xo, p)], k_recv.at[p])
    for p in range(len(cuts)):
        for l in range(spc):
            side[x, l, :, span(xo, p)] = kern[owners[l] % (2 * nk), :, span(xo, p)]
        src = side.at[x, 0, :, span(xo, p)]
        send(src, src, e_recv.at[0, p], x_peer, "core")
    for l in range(1, spc):
        for p in range(len(cuts)):
            src = side.at[x, l, :, span(xo, p)]
            send(src, src, e_recv.at[l, p], x_peer, "core")

    half = n // 2
    wide_lane = m // 2
    src_lane = lax.broadcasted_iota(jnp.int32, (half, half), 0)
    dst_lane = lax.broadcasted_iota(jnp.int32, (half, half), 1)
    perm = jnp.where((src_lane % wide_lane) * radix + src_lane // wide_lane == dst_lane, 1.0, 0.0).astype(BF)
    lane_perm[:half] = perm
    lane_perm[half:] = perm

    def own(l, p):
        arrive(side.at[xo, l, :, span(x, p)], e_recv.at[l, p])
        mine = owners[l] // (2 * nk) == x
        held[l, z, y, :, span(x, p)] = jnp.where(mine, side[x, l, :, span(x, p)], side[xo, l, :, span(x, p)])
        if p in parts:
            here = piece(l, z, y, x, p)
            send(here, here, y_recv.at[l, z, p], y_peer, "core")
            send(here, here, z_recv.at[l, z, p], at_z(z - 1), "down", z > 0)
            send(here, here, z_recv.at[l, z, p], at_z(z + 1), "up", z < nz - 1)

    def across(l, p):
        here = piece(l, z, yo, x, p)
        send(here, here, y_recv.at[l, z, p], at_z(z - 1), "down", z > 0)
        send(here, here, y_recv.at[l, z, p], at_z(z + 1), "up", z < nz - 1)

    def share_x(l, zz, yy, group, cond=None):
        if share:
            here = piece(l, zz, yy, x, 0)
            send(here, here, x_recv.at[l, zz, yy], x_peer, group, cond)

    def z_in(l, j, p):
        for s, zz, have, dest, more in ((1, z + j, z + j < nz, z - 1, z > 0), (-1, z - j, z >= j, z + 1, z < nz - 1)):
            here = piece(l, zz, y, x, p)
            pl.when(have)(functools.partial(arrive, here, z_recv.at[l, zz, p]))
            if j < nz - 1:
                send(here, here, z_recv.at[l, zz, p], at_z(dest), ("relay", s * j), have & more)
            if l != last or j > 1:
                send(here, here, y_recv.at[l, zz, p], y_peer, ("on", s * j), have)
            if p == 0:
                share_x(l, zz, y, ("on", s * j), have)

    def y_in(l, j, p):
        if j == 0:
            arrive(piece(l, z, yo, x, p), y_recv.at[l, z, p])
            if p == 0:
                share_x(l, z, yo, "core")
            return
        for s, zz, have in ((1, z + j, z + j < nz), (-1, z - j, z >= j)):
            pl.when(have)(functools.partial(arrive, piece(l, zz, yo, x, p), y_recv.at[l, zz, p]))
            if p == 0:
                share_x(l, zz, yo, ("on", s * j), have)

    def near(k):
        if k == 0:
            return z
        low = jnp.minimum(z, nz - 1 - z)
        both = z + (k + 1) // 2 if k % 2 else z - k // 2
        one = jnp.where(low == z, z + k - low, z - k + low)
        return jnp.where(k <= 2 * low, both, one)

    def x_in(l, k, yy):
        if share and not (k == 0 and yy is y):
            arrive(piece(l, near(k), yy, xo, 0), x_recv.at[l, near(k), yy])

    strip = 16
    waiting = []
    ready = []

    def product(l, k, yy, slot, tile, strip_index):
        zi = near(k)
        lo_row = strip * strip_index
        at = pl.ds(pl.multiple_of((2 * zi + yy) * rows + lo_row, strip), strip)
        src = slice(lo_row, lo_row + strip)
        to = slice(tile * rows + lo_row, tile * rows + lo_row + strip)
        re, im = [], []
        for q in range(radix):
            lanes = slice(q * m, (q + 1) * m)
            kr, ki = held[l, zi, yy, 0, src, lanes], held[l, zi, yy, 1, src, lanes]
            mr, mi = mask[tile, 0, at, lanes], mask[tile, 1, at, lanes]
            re.append(mr * kr - mi * ki)
            im.append(mr * ki + mi * kr)
        for r, pair in enumerate(radix4(re, im)):
            for p, v in enumerate(pair):
                hi, lo = split(v)
                stage[slot, r, to, p * m:(p + 1) * m] = hi
                stage[slot, r, to, (2 + p) * m:(3 + p) * m] = lo

    def row_matmul(l, k, yy, slot, r):
        hi, lo = stage[slot, r, :, :2 * m], stage[slot, r, :, 2 * m:]
        th, tl = rowt[r, :2 * m], rowt[r, 2 * m:]
        done = jnp.dot(jnp.concatenate([hi, lo, hi], 1), jnp.concatenate([th, th, tl], 0),
                       preferred_element_type=F32)
        at = pl.ds(pl.multiple_of((2 * near(k) + yy) * rows, rows), rows)
        for tile in range(2):
            field[l, r, tile, at] = done[tile * rows:(tile + 1) * rows]

    def woven(first, second):
        count = max(len(first), len(second))
        for i in range(count):
            for group in (first, second):
                for work in group[i * len(group) // count:(i + 1) * len(group) // count]:
                    work()

    def held_matmuls():
        works = [functools.partial(row_matmul, *waiting[0], r) for r in range(radix)] if waiting else []
        waiting.clear()
        return works

    def row_step(l, k, other):
        yy = yo if other else y
        x_in(l, k, yy)
        slot = 1 - waiting[0][3] if waiting else 0
        products = [functools.partial(product, l, k, yy, slot, tile, i)
                    for i in range(rows // strip) for tile in range(2)]
        woven(held_matmuls(), products)
        waiting.append((l, k, yy, slot))

    def middle(l, tile, ry):
        def strip_of(i):
            base = i * strip
            lanes = slice(ry * m, (ry + 1) * m)
            re = [field[l, ry, tile, k * m + base:k * m + base + strip, :m] for k in range(radix)]
            im = [field[l, ry, tile, k * m + base:k * m + base + strip, m:] for k in range(radix)]
            for rx, pair in enumerate(radix4(re, im)):
                for p, v in enumerate(pair):
                    hi, lo = split(v)
                    cols[tile, rx, p * m + base:p * m + base + strip, lanes] = hi
                    cols[tile, rx, (2 + p) * m + base:(2 + p) * m + base + strip, lanes] = lo
        return [functools.partial(strip_of, i) for i in range(m // strip)]

    def columns(l, tile, rx):
        hi, lo = cols[tile, rx, :2 * m], cols[tile, rx, 2 * m:]
        th, tl = colt[rx, :, :2 * m], colt[rx, :, 2 * m:]
        done = jnp.dot(jnp.concatenate([th, th, tl], 1), jnp.concatenate([hi, lo, hi], 0),
                       preferred_element_type=F32)
        power = (done[:m] * done[:m] + done[m:] * done[m:]) * weight_ref[c * spc + l]
        if l == 0:
            total[tile, rx] = power
        else:
            total[tile, rx] += power

    def column_step(l, tile, rx):
        if rx == 0 and waiting and waiting[0][0] == l:
            woven(held_matmuls(), [])
        if rx == 0 and (l, tile) not in ready:
            for ry in range(radix):
                woven(middle(l, tile, ry), [])
        woven([functools.partial(columns, l, tile, rx)], middle(l, 1 - tile, rx) if tile == 1 else [])
        if tile == 1:
            ready.append((l, 0))
        if l == last and tile == 1:
            for done in [rx - 1] if rx < radix - 1 else [rx - 1, rx]:
                if done >= 0:
                    send(total.at[1, done], part.at[done], p_recv.at[0], c_peer, "part")

    steps = (own, z_in, y_in, across, row_step, column_step)
    first_row = True
    for op, *args in program(spc, nz, len(cuts), parts, radix):
        if op == 4 and first_row:
            first_row = False
            for load in loads[1:]:
                load.wait()
            arrive(mask.at[1], m_recv.at[0])
        steps[op](*args)

    arrive(part, p_recv.at[0])
    low = lax.broadcasted_iota(jnp.int32, (m, m), 1) < wide_lane
    perm = lane_perm[...]
    for rx in range(radix):
        lanes = [total[0, rx, :, r * m:(r + 1) * m] + part[rx, :, r * m:(r + 1) * m] for r in range(radix)]
        turned = [pltpu.roll(v, wide_lane, 1) for v in lanes]
        for h in range(2):
            pairs = [jnp.where(low, *((lanes[r], turned[r + 1]) if h == 0 else (turned[r], lanes[r + 1])))
                     for r in range(0, radix, 2)]
            hi, lo = split(jnp.concatenate(pairs, 1))
            image = jnp.dot(jnp.concatenate([hi, lo], 1), perm, preferred_element_type=F32)
            for q in range(radix // 2):
                blocks[h * (radix // 2) + q, pl.ds(rx, m, stride=radix), :] = image[:, q * m:(q + 1) * m]
    for q in range(radix):
        out_ref[:, q * m:(q + 1) * m] = blocks[q]
    all_gone()


def local(mesh_shape, mask_spectrum, kernels, owner_table, step_weight):
    groups, tiles = mesh_shape
    nk, _, rows, n = kernels.shape
    steps = owner_table.shape[0]
    radix = 4
    m = n // radix
    spc = steps // 2
    nz = tiles // 2
    most = min(rows // 8, 4)
    rowt, colt = tables(n, radix)
    dma = pltpu.SemaphoreType.DMA
    any_spec = pl.BlockSpec(memory_space=pl.ANY)
    smem = pl.BlockSpec(memory_space=pltpu.SMEM)
    out = pl.pallas_call(
        functools.partial(kernel, (spc, nk, nz, rows, n, radix)),
        out_shape=pltpu.VMEM((n, n), F32),
        in_specs=[smem, smem, any_spec, any_spec, any_spec, any_spec],
        out_specs=pl.BlockSpec(memory_space=pltpu.VMEM),
        scratch_shapes=[
            pltpu.VMEM((2 * nk, 2, rows, n), F32),
            pltpu.VMEM((2, spc, 2, rows, n), F32),
            pltpu.VMEM((spc, nz, 2, 2, rows, n), F32),
            pltpu.VMEM((2, 2, n, n), F32),
            pltpu.VMEM(rowt.shape, BF),
            pltpu.VMEM(colt.shape, BF),
            pltpu.VMEM((n, n // 2), BF),
            pltpu.VMEM((2, radix, 2 * rows, 4 * m), BF),
            pltpu.VMEM((spc, radix, 2, n, 2 * m), F32),
            pltpu.VMEM((2, radix, 4 * m, n), BF),
            pltpu.VMEM((2, radix, m, n), F32),
            pltpu.VMEM((radix, m, n), F32),
            pltpu.VMEM((radix, n, m), F32),
            dma((4,)), dma((most,)), dma((1,)), dma((spc, most)), dma((spc, nz, most)), dma((spc, nz, most)),
            dma((spc, nz, 2)), dma((1,)), dma((4 * nz + 2,)),
        ],
        compiler_params=pltpu.CompilerParams(collective_id=0, has_side_effects=True, vmem_limit_bytes=54 * 1024 * 1024),
    )(owner_table, step_weight, mask_spectrum[0], kernels, jnp.asarray(rowt), jnp.asarray(colt))
    return out[None]


def solution(mesh):
    in_specs = (P(("kgrp", "tile"), None, None, None), P("kgrp", None, "tile", None), P(), P())
    out_specs = P(("kgrp", "tile"), None, None)
    body = functools.partial(local, (mesh.shape["kgrp"], mesh.shape["tile"]))
    return jax.shard_map(body, mesh=mesh, in_specs=in_specs, out_specs=out_specs, check_vma=False)
```

time: 56.5 us -> 50.2 us (0.89)
  Pallas kernels: 54.1 us -> 48.7 us
  local copies, waits for them, and re-layouts: 2.26 us -> 0.97 us
    pallas_call x1, Pallas kernels: 54.1 us -> 48.7 us  [local(): pl.pallas_call(functools.partial(kernel, (spc, nk, nz, rows, n, radix)),...]
    unnamed x1, local copies, waits for them, and re-layouts: 2.26 us -> 0.97 us
where the time goes in v2:
time: 50.2 us; the launch traced here: 49.6 us
  Pallas kernels  48.7 us (97%)
  local copies, waits for them, and re-layouts  0.97 us (2%)
    pallas_call x1, Pallas kernels, local(): pl.pallas_call(functools.partial(kernel, (spc, nk, nz, rows, n, radix)),...  48.7 us

profile of v2, /device:TPU:0, one launch (start us, length us, event | category | flops | bytes accessed | tf_op | source)
XLA Modules:
  0.0 49.6 jit_solution(11050955152168445887)
XLA Ops:
  0.0 48.7 %shard_map.64 = f32[512,512]{1,0:T(8,128)S(1)} custom-call(s32[4]{0:T(128)} %owner_ref.1, f32[4]{0:T(128)} %weight_ref.1, f32[2,512,512]{2,1,0:T(8,128)} %bitcast.3, f32[2,2,64,512]{3,2,1,0:T(8,128)} %kern_hbm.1, bf16[4,512,256]{2,1,0:T(8,128)(2,1)} %constant.4.clone.rowt_hbm, bf16[4,256,512]{2,1,0:T(8,128)(2,1)} %constant.5.clone.colt_hbm), custom_call_target="tpu_custom_call" | custom-call | tf_op jit(solution)/shard_map/pallas_call | solution.py:385
  48.7 1.0 %copy.8 = f32[1,512,512]{2,1,0:T(8,128)} copy(f32[1,512,512]{2,1,0:T(8,128)S(1)} %bitcast.2) | data formatting | bytes 2097152

commit v3 on v2

--- a/solution.py
+++ b/solution.py
@@ -21,18 +21,23 @@
     return hi, lo
 
 
-def tables(n, radix):
+def tables(n, radix, rows):
     m = n // radix
     a = np.arange(m)
-    rows = []
+    blocks = []
     for r in range(radix):
         phase = (a[:, None] * (r + radix * a[None, :])) % n * (2.0 * math.pi / n)
         c, s = np.cos(phase) / math.sqrt(n), np.sin(phase) / math.sqrt(n)
-        rows.append(np.block([[c, s], [-s, c]]))
-    b = np.stack(rows)
+        blocks.append(np.block([[c, s], [-s, c]]))
+    b = np.stack(blocks)
     bh, bl = split_np(b)
     row = np.concatenate([bh, bl], axis=1)
-    col = np.concatenate([bh.transpose(0, 2, 1), bl.transpose(0, 2, 1)], axis=2)
+    halves = []
+    for parity in (0, 1):
+        pick = a[(a // rows) % 2 == parity]
+        pick = np.concatenate([pick, m + pick])
+        halves.append(np.concatenate([bh.transpose(0, 2, 1)[:, :, pick], bl.transpose(0, 2, 1)[:, :, pick]], axis=2))
+    col = np.stack(halves, axis=1)
     return row, col
 
 
@@ -50,17 +55,19 @@
 OWN, Z_IN, Y_IN, ACROSS, ROWS, COLUMNS = range(6)
 TUNED = {
     (2, 4, 4, 3, 4): [
-        (0, 0, 0), (0, 0, 1), (0, 0, 2), (1, 0, 1, 0), (0, 1, 0), (1, 0, 1, 1), (1, 0, 2, 0), (0, 0, 3),
-        (2, 0, 1, 0), (1, 0, 1, 2), (1, 0, 2, 1), (1, 0, 3, 0), (1, 0, 2, 2), (0, 1, 1), (4, 0, 2, 0), (2, 0, 0, 0),
-        (4, 0, 1, 0), (4, 0, 0, 0), (1, 1, 1, 0), (2, 0, 2, 0), (2, 0, 0, 1), (2, 1, 0, 0), (1, 0, 3, 1), (0, 1, 2),
-        (1, 0, 3, 2), (1, 1, 1, 1), (2, 0, 1, 1), (4, 0, 3, 0), (2, 0, 3, 0), (2, 0, 0, 2), (4, 0, 0, 1), (2, 0, 3, 1),
-        (1, 1, 2, 0), (1, 1, 1, 2), (0, 1, 3), (2, 0, 2, 1), (2, 0, 1, 2), (3, 1, 0), (4, 1, 0, 0), (1, 1, 3, 0),
-        (2, 0, 2, 2), (4, 1, 1, 0), (4, 0, 2, 1), (2, 0, 3, 2), (4, 0, 3, 1), (1, 1, 2, 1), (2, 1, 0, 1), (1, 1, 2, 2),
-        (3, 1, 1), (2, 1, 0, 2), (4, 0, 1, 1), (3, 1, 2), (2, 1, 1, 0), (4, 1, 2, 0), (5, 0, 1, 0), (2, 1, 2, 0),
-        (5, 0, 1, 1), (1, 1, 3, 1), (4, 1, 0, 1), (5, 0, 1, 2), (5, 0, 1, 3), (2, 1, 2, 1), (2, 1, 3, 0), (1, 1, 3, 2),
-        (5, 0, 0, 0), (5, 0, 0, 1), (2, 1, 1, 1), (5, 0, 0, 2), (4, 1, 3, 0), (2, 1, 3, 1), (2, 1, 2, 2), (5, 0, 0, 3),
-        (2, 1, 1, 2), (4, 1, 1, 1), (4, 1, 2, 1), (2, 1, 3, 2), (4, 1, 3, 1), (5, 1, 1, 0), (5, 1, 1, 1), (5, 1, 1, 2),
-        (5, 1, 1, 3), (5, 1, 0, 0), (5, 1, 0, 1), (5, 1, 0, 2), (5, 1, 0, 3),
+        (0, 0, 0), (0, 0, 1), (0, 0, 2), (2, 0, 0, 0), (1, 0, 1, 0), (0, 1, 0), (1, 0, 1, 1), (1, 0, 2, 0),
+        (1, 0, 1, 2), (0, 1, 1), (0, 0, 3), (1, 0, 3, 0), (1, 0, 2, 1), (2, 0, 1, 0), (1, 0, 2, 2), (4, 0, 1, 0),
+        (1, 1, 1, 0), (1, 0, 3, 1), (0, 1, 2), (2, 0, 3, 0), (1, 0, 3, 2), (4, 0, 2, 0), (4, 0, 0, 0), (4, 0, 3, 0),
+        (2, 0, 2, 0), (2, 0, 0, 1), (5, 0, 1, 0, 0), (2, 0, 1, 1), (5, 0, 1, 1, 0), (0, 1, 3), (5, 0, 1, 2, 0), (5, 0, 1, 3, 0),
+        (2, 0, 1, 2), (1, 1, 1, 1), (1, 1, 2, 0), (2, 0, 3, 1), (2, 1, 0, 0), (2, 1, 0, 1), (1, 1, 1, 2), (2, 0, 0, 2),
+        (4, 1, 1, 0), (5, 0, 0, 0, 0), (3, 1, 0), (4, 0, 1, 1), (4, 0, 0, 1), (1, 1, 2, 1), (2, 0, 2, 1), (2, 0, 2, 2),
+        (4, 1, 0, 0), (5, 0, 0, 1, 0), (2, 0, 3, 2), (1, 1, 3, 0), (5, 0, 0, 2, 0), (5, 0, 0, 3, 0), (2, 1, 0, 2), (4, 0, 2, 1),
+        (4, 0, 3, 1), (1, 1, 2, 2), (5, 0, 1, 0, 1), (5, 0, 1, 1, 1), (3, 1, 1), (2, 1, 2, 0), (4, 1, 2, 0), (4, 1, 0, 1),
+        (5, 0, 1, 2, 1), (2, 1, 1, 0), (5, 0, 1, 3, 1), (5, 0, 0, 0, 1), (3, 1, 2), (2, 1, 2, 1), (1, 1, 3, 1), (5, 0, 0, 1, 1),
+        (2, 1, 3, 0), (5, 0, 0, 2, 1), (5, 0, 0, 3, 1), (1, 1, 3, 2), (4, 1, 3, 0), (2, 1, 2, 2), (5, 1, 1, 0, 0), (5, 1, 1, 1, 0),
+        (5, 1, 1, 2, 0), (5, 1, 1, 3, 0), (2, 1, 3, 1), (5, 1, 0, 0, 0), (5, 1, 0, 1, 0), (5, 1, 0, 2, 0), (2, 1, 1, 1), (5, 1, 0, 3, 0),
+        (2, 1, 1, 2), (4, 1, 1, 1), (2, 1, 3, 2), (4, 1, 2, 1), (4, 1, 3, 1), (5, 1, 1, 0, 1), (5, 1, 1, 1, 1), (5, 1, 1, 2, 1),
+        (5, 1, 1, 3, 1), (5, 1, 0, 0, 1), (5, 1, 0, 1, 1), (5, 1, 0, 2, 1), (5, 1, 0, 3, 1),
     ],
 }
 
@@ -79,13 +86,13 @@
         order += [(ACROSS, l, p) for p in parts if end]
         order += [(Y_IN, l, 1, p) for p in parts if end]
         order += [(ROWS, l, k, other) for k in range(nz) for other in (0, 1)]
-        order += [(COLUMNS, l, tile, rx) for tile in (1, 0) for rx in range(radix)]
+        order += [(COLUMNS, l, tile, rx, phase) for phase in (0, 1) for tile in (1, 0) for rx in range(radix)]
     return order
 
 
 def kernel(dims, owner_ref, weight_ref, mask_hbm, kern_hbm, rowt_hbm, colt_hbm, out_ref,
-           kern, side, held, mask, rowt, colt, lane_perm, stage, field, cols, total, part, blocks,
-           loc, k_recv, m_recv, e_recv, z_recv, y_recv, x_recv, p_recv, gone):
+           side, held, mask, rowt, colt, lane_perm, stage, field, cols, acc, total, part, blocks,
+           loc, k_recv, m_recv, e_recv, z_recv, y_recv, x_recv, p_recv, gone, *kern):
     spc, nk, nz, rows, n, radix = dims
     m = n // radix
     last = spc - 1
@@ -108,8 +115,7 @@
     cuts = [(i, i + wide) for i in range(0, nt, wide)]
     parts = [p for p, cut in enumerate(cuts) if cut[1] <= keep]
 
-    def span(s, p):
-        a, b = cuts[p]
+    def tiles_of(s, a, b):
         return pl.ds(pl.multiple_of(a * unit + s * (rows - unit * (a + b)), unit), unit * (b - a))
 
     barrier = pltpu.get_barrier_semaphore()
@@ -124,16 +130,27 @@
     def _():
         pl.semaphore_signal(barrier, inc=1, device_id=at_z(z + 1), device_id_type=MESH)
 
-    own_kern = kern.at[pl.ds(c * nk, nk)]
+    def span(s, p):
+        return tiles_of(s, *cuts[p])
+
+    def pieces_of(l, p):
+        a, b = cuts[p]
+        return [(a, a + 1), (a + 1, b)] if l == p == 0 and b - a > 1 else [(a, b)]
+
+    def candidates(core, p):
+        return kern[p].at[pl.ds(core * nk, nk)]
+
+    first_loads = [pltpu.make_async_copy(kern_hbm.at[:, :, span(xo, p)], candidates(c, p), loc.at[3 + p])
+                   for p in range(len(cuts))]
     loads = [
-        pltpu.make_async_copy(kern_hbm, own_kern, loc.at[0]),
-        pltpu.make_async_copy(mask_hbm, mask.at[0], loc.at[1]),
-        pltpu.make_async_copy(rowt_hbm, rowt, loc.at[2]),
-        pltpu.make_async_copy(colt_hbm, colt, loc.at[3]),
+        pltpu.make_async_copy(mask_hbm, mask.at[0], loc.at[0]),
+        pltpu.make_async_copy(rowt_hbm, rowt, loc.at[1]),
+        pltpu.make_async_copy(colt_hbm, colt, loc.at[2]),
     ]
-    for load in loads:
+    for load in first_loads + loads:
         load.start()
-    loads[0].wait()
+    for load in first_loads:
+        load.wait()
     pl.semaphore_wait(barrier, 3 + jnp.minimum(z, 1) + jnp.minimum(nz - 1 - z, 1))
 
     groups = {}
@@ -171,18 +188,18 @@
         return held.at[l, zz, yy, :, span(s, p)]
 
     for p in range(len(cuts)):
-        src = kern.at[pl.ds(c * nk, nk), :, span(xo, p)]
+        src = candidates(c, p)
         send(src, src, k_recv.at[p], c_peer, "core")
     send(mask_hbm, mask.at[1], m_recv.at[0], c_peer, "mask")
 
     owners = [owner_ref[c * spc + l] for l in range(spc)]
     for p in range(len(cuts)):
-        arrive(kern.at[pl.ds(co * nk, nk), :, span(xo, p)], k_recv.at[p])
-    for p in range(len(cuts)):
+        arrive(candidates(co, p), k_recv.at[p])
         for l in range(spc):
-            side[x, l, :, span(xo, p)] = kern[owners[l] % (2 * nk), :, span(xo, p)]
-        src = side.at[x, 0, :, span(xo, p)]
-        send(src, src, e_recv.at[0, p], x_peer, "core")
+            side[x, l, :, span(xo, p)] = kern[p][owners[l] % (2 * nk)]
+        for i, sub in enumerate(pieces_of(0, p)):
+            src = side.at[x, 0, :, tiles_of(xo, *sub)]
+            send(src, src, e_recv.at[0, p + (len(cuts) if i else 0)], x_peer, "core")
     for l in range(1, spc):
         for p in range(len(cuts)):
             src = side.at[x, l, :, span(xo, p)]
@@ -197,14 +214,16 @@
     lane_perm[half:] = perm
 
     def own(l, p):
-        arrive(side.at[xo, l, :, span(x, p)], e_recv.at[l, p])
         mine = owners[l] // (2 * nk) == x
-        held[l, z, y, :, span(x, p)] = jnp.where(mine, side[x, l, :, span(x, p)], side[xo, l, :, span(x, p)])
-        if p in parts:
-            here = piece(l, z, y, x, p)
-            send(here, here, y_recv.at[l, z, p], y_peer, "core")
-            send(here, here, z_recv.at[l, z, p], at_z(z - 1), "down", z > 0)
-            send(here, here, z_recv.at[l, z, p], at_z(z + 1), "up", z < nz - 1)
+        for i, sub in enumerate(pieces_of(l, p)):
+            at = tiles_of(x, *sub)
+            arrive(side.at[xo, l, :, at], e_recv.at[l, p + (len(cuts) if i else 0)])
+            held[l, z, y, :, at] = jnp.where(mine, side[x, l, :, at], side[xo, l, :, at])
+            if p in parts:
+                here = held.at[l, z, y, :, at]
+                send(here, here, y_recv.at[l, z, p], y_peer, "core")
+                send(here, here, z_recv.at[l, z, p], at_z(z - 1), "down", z > 0)
+                send(here, here, z_recv.at[l, z, p], at_z(z + 1), "up", z < nz - 1)
 
     def across(l, p):
         here = piece(l, z, yo, x, p)
@@ -252,7 +271,6 @@
 
     strip = 16
     waiting = []
-    ready = []
 
     def product(l, k, yy, slot, tile, strip_index):
         zi = near(k)
@@ -303,40 +321,48 @@
         woven(held_matmuls(), products)
         waiting.append((l, k, yy, slot))
 
-    def middle(l, tile, ry):
+    def middle(l, tile, ry, phase):
+        own_half = y if phase == 0 else yo
+
         def strip_of(i):
-            base = i * strip
+            at = strip * i
+            base = at // rows * 2 * rows + at % rows
             lanes = slice(ry * m, (ry + 1) * m)
-            re = [field[l, ry, tile, k * m + base:k * m + base + strip, :m] for k in range(radix)]
-            im = [field[l, ry, tile, k * m + base:k * m + base + strip, m:] for k in range(radix)]
+            from_rows = [pl.ds(pl.multiple_of(k * m + base + own_half * rows, strip), strip) for k in range(radix)]
+            re = [field[l, ry, tile, rows_at, :m] for rows_at in from_rows]
+            im = [field[l, ry, tile, rows_at, m:] for rows_at in from_rows]
             for rx, pair in enumerate(radix4(re, im)):
                 for p, v in enumerate(pair):
                     hi, lo = split(v)
-                    cols[tile, rx, p * m + base:p * m + base + strip, lanes] = hi
-                    cols[tile, rx, (2 + p) * m + base:(2 + p) * m + base + strip, lanes] = lo
-        return [functools.partial(strip_of, i) for i in range(m // strip)]
-
-    def columns(l, tile, rx):
-        hi, lo = cols[tile, rx, :2 * m], cols[tile, rx, 2 * m:]
-        th, tl = colt[rx, :, :2 * m], colt[rx, :, 2 * m:]
-        done = jnp.dot(jnp.concatenate([th, th, tl], 1), jnp.concatenate([hi, lo, hi], 0),
-                       preferred_element_type=F32)
+                    to = p * (m // 2) + at
+                    cols[tile, rx, to:to + strip, lanes] = hi
+                    cols[tile, rx, m + to:m + to + strip, lanes] = lo
+        return [functools.partial(strip_of, i) for i in range(m // 2 // strip)]
+
+    def columns(l, tile, rx, phase):
+        hi, lo = cols[tile, rx, :m], cols[tile, rx, m:]
+        own_half = y if phase == 0 else yo
+        th, tl = colt[rx, own_half, :, :m], colt[rx, own_half, :, m:]
+        done = (jnp.dot(jnp.concatenate([th, tl], 1), jnp.concatenate([hi, hi], 0), preferred_element_type=F32)
+                + jnp.dot(th, lo, preferred_element_type=F32))
+        if phase == 0:
+            acc[tile, rx] = done
+            return
+        done += acc[tile, rx]
         power = (done[:m] * done[:m] + done[m:] * done[m:]) * weight_ref[c * spc + l]
         if l == 0:
             total[tile, rx] = power
         else:
             total[tile, rx] += power
 
-    def column_step(l, tile, rx):
+    def column_step(l, tile, rx, phase):
         if rx == 0 and waiting and waiting[0][0] == l:
             woven(held_matmuls(), [])
-        if rx == 0 and (l, tile) not in ready:
+        if rx == 0 and tile == 1:
             for ry in range(radix):
-                woven(middle(l, tile, ry), [])
-        woven([functools.partial(columns, l, tile, rx)], middle(l, 1 - tile, rx) if tile == 1 else [])
-        if tile == 1:
-            ready.append((l, 0))
-        if l == last and tile == 1:
+                woven(middle(l, tile, ry, phase), [])
+        woven([functools.partial(columns, l, tile, rx, phase)], middle(l, 0, rx, phase) if tile == 1 else [])
+        if l == last and tile == 1 and phase == 1:
             for done in [rx - 1] if rx < radix - 1 else [rx - 1, rx]:
                 if done >= 0:
                     send(total.at[1, done], part.at[done], p_recv.at[0], c_peer, "part")
@@ -346,7 +372,7 @@
     for op, *args in program(spc, nz, len(cuts), parts, radix):
         if op == 4 and first_row:
             first_row = False
-            for load in loads[1:]:
+            for load in loads:
                 load.wait()
             arrive(mask.at[1], m_recv.at[0])
         steps[op](*args)
@@ -378,7 +404,8 @@
     spc = steps // 2
     nz = tiles // 2
     most = min(rows // 8, 4)
-    rowt, colt = tables(n, radix)
+    kept = most - (rows // 8 >= 4)
+    rowt, colt = tables(n, radix, rows)
     dma = pltpu.SemaphoreType.DMA
     any_spec = pl.BlockSpec(memory_space=pl.ANY)
     smem = pl.BlockSpec(memory_space=pltpu.SMEM)
@@ -388,7 +415,6 @@
         in_specs=[smem, smem, any_spec, any_spec, any_spec, any_spec],
         out_specs=pl.BlockSpec(memory_space=pltpu.VMEM),
         scratch_shapes=[
-            pltpu.VMEM((2 * nk, 2, rows, n), F32),
             pltpu.VMEM((2, spc, 2, rows, n), F32),
             pltpu.VMEM((spc, nz, 2, 2, rows, n), F32),
             pltpu.VMEM((2, 2, n, n), F32),
@@ -397,13 +423,14 @@
             pltpu.VMEM((n, n // 2), BF),
             pltpu.VMEM((2, radix, 2 * rows, 4 * m), BF),
             pltpu.VMEM((spc, radix, 2, n, 2 * m), F32),
-            pltpu.VMEM((2, radix, 4 * m, n), BF),
+            pltpu.VMEM((2, radix, 2 * m, n), BF),
+            pltpu.VMEM((2, radix, 2 * m, n), F32),
             pltpu.VMEM((2, radix, m, n), F32),
             pltpu.VMEM((radix, m, n), F32),
             pltpu.VMEM((radix, n, m), F32),
-            dma((4,)), dma((most,)), dma((1,)), dma((spc, most)), dma((spc, nz, most)), dma((spc, nz, most)),
+            dma((3 + most,)), dma((most,)), dma((1,)), dma((spc, most + 1)), dma((spc, nz, kept)), dma((spc, nz, kept)),
             dma((spc, nz, 2)), dma((1,)), dma((4 * nz + 2,)),
-        ],
+        ] + [pltpu.VMEM((2 * nk, 2, rows // most, n), F32)] * most,
         compiler_params=pltpu.CompilerParams(collective_id=0, has_side_effects=True, vmem_limit_bytes=54 * 1024 * 1024),
     )(owner_table, step_weight, mask_spectrum[0], kernels, jnp.asarray(rowt), jnp.asarray(colt))
     return out[None]

time: 50.2 us -> 48.8 us (0.972)
  Pallas kernels: 48.7 us -> 47.2 us
    pallas_call x1, Pallas kernels: 48.7 us -> 47.2 us  [local(): pl.pallas_call(functools.partial(kernel, (spc, nk, nz, rows, n, radix)),...]
where the time goes in v3:
time: 48.8 us; the launch traced here: 48.1 us
  Pallas kernels  47.2 us (97%)
  local copies, waits for them, and re-layouts  0.97 us (2%)
    pallas_call x1, Pallas kernels, local(): pl.pallas_call(functools.partial(kernel, (spc, nk, nz, rows, n, radix)),...  47.2 us

profile of v3, /device:TPU:0, one launch (start us, length us, event | category | flops | bytes accessed | tf_op | source)
XLA Modules:
  0.0 48.1 jit_solution(6916009765685681340)
XLA Ops:
  0.0 47.2 %shard_map.64 = f32[512,512]{1,0:T(8,128)S(1)} custom-call(s32[4]{0:T(128)} %owner_ref.1, f32[4]{0:T(128)} %weight_ref.1, f32[2,512,512]{2,1,0:T(8,128)} %bitcast.3, f32[2,2,64,512]{3,2,1,0:T(8,128)} %kern_hbm.1, bf16[4,512,256]{2,1,0:T(8,128)(2,1)} %constant.4.clone.rowt_hbm, bf16[4,2,256,256]{3,2,1,0:T(8,128)(2,1)} %constant.5.clone.colt_hbm), custom_call_target="tpu_custom_call" | custom-call | tf_op jit(solution)/shard_map/pallas_call | solution.py:412
  47.2 1.0 %copy.8 = f32[1,512,512]{2,1,0:T(8,128)} copy(f32[1,512,512]{2,1,0:T(8,128)S(1)} %bitcast.2) | data formatting | bytes 2097152

commit v4 on v3

--- a/solution.py
+++ b/solution.py
@@ -55,18 +55,18 @@
 OWN, Z_IN, Y_IN, ACROSS, ROWS, COLUMNS = range(6)
 TUNED = {
     (2, 4, 4, 3, 4): [
-        (0, 0, 0), (0, 0, 1), (0, 0, 2), (2, 0, 0, 0), (1, 0, 1, 0), (0, 1, 0), (1, 0, 1, 1), (1, 0, 2, 0),
-        (1, 0, 1, 2), (0, 1, 1), (0, 0, 3), (1, 0, 3, 0), (1, 0, 2, 1), (2, 0, 1, 0), (1, 0, 2, 2), (4, 0, 1, 0),
-        (1, 1, 1, 0), (1, 0, 3, 1), (0, 1, 2), (2, 0, 3, 0), (1, 0, 3, 2), (4, 0, 2, 0), (4, 0, 0, 0), (4, 0, 3, 0),
-        (2, 0, 2, 0), (2, 0, 0, 1), (5, 0, 1, 0, 0), (2, 0, 1, 1), (5, 0, 1, 1, 0), (0, 1, 3), (5, 0, 1, 2, 0), (5, 0, 1, 3, 0),
-        (2, 0, 1, 2), (1, 1, 1, 1), (1, 1, 2, 0), (2, 0, 3, 1), (2, 1, 0, 0), (2, 1, 0, 1), (1, 1, 1, 2), (2, 0, 0, 2),
-        (4, 1, 1, 0), (5, 0, 0, 0, 0), (3, 1, 0), (4, 0, 1, 1), (4, 0, 0, 1), (1, 1, 2, 1), (2, 0, 2, 1), (2, 0, 2, 2),
-        (4, 1, 0, 0), (5, 0, 0, 1, 0), (2, 0, 3, 2), (1, 1, 3, 0), (5, 0, 0, 2, 0), (5, 0, 0, 3, 0), (2, 1, 0, 2), (4, 0, 2, 1),
-        (4, 0, 3, 1), (1, 1, 2, 2), (5, 0, 1, 0, 1), (5, 0, 1, 1, 1), (3, 1, 1), (2, 1, 2, 0), (4, 1, 2, 0), (4, 1, 0, 1),
-        (5, 0, 1, 2, 1), (2, 1, 1, 0), (5, 0, 1, 3, 1), (5, 0, 0, 0, 1), (3, 1, 2), (2, 1, 2, 1), (1, 1, 3, 1), (5, 0, 0, 1, 1),
-        (2, 1, 3, 0), (5, 0, 0, 2, 1), (5, 0, 0, 3, 1), (1, 1, 3, 2), (4, 1, 3, 0), (2, 1, 2, 2), (5, 1, 1, 0, 0), (5, 1, 1, 1, 0),
-        (5, 1, 1, 2, 0), (5, 1, 1, 3, 0), (2, 1, 3, 1), (5, 1, 0, 0, 0), (5, 1, 0, 1, 0), (5, 1, 0, 2, 0), (2, 1, 1, 1), (5, 1, 0, 3, 0),
-        (2, 1, 1, 2), (4, 1, 1, 1), (2, 1, 3, 2), (4, 1, 2, 1), (4, 1, 3, 1), (5, 1, 1, 0, 1), (5, 1, 1, 1, 1), (5, 1, 1, 2, 1),
+        (0, 0, 0), (0, 0, 1), (0, 0, 2), (1, 0, 1, 0), (1, 0, 1, 1), (0, 1, 0), (1, 0, 2, 0), (1, 0, 1, 2),
+        (0, 0, 3), (1, 0, 2, 1), (2, 0, 1, 0), (1, 0, 3, 0), (1, 0, 2, 2), (2, 0, 0, 0), (2, 0, 0, 1), (0, 1, 1),
+        (4, 0, 2, 0), (1, 0, 3, 1), (2, 0, 0, 2), (1, 1, 1, 0), (0, 1, 2), (2, 0, 3, 0), (2, 0, 1, 1), (2, 0, 2, 0),
+        (2, 1, 0, 0), (1, 0, 3, 2), (4, 0, 3, 0), (4, 0, 1, 0), (4, 0, 0, 0), (1, 1, 2, 0), (1, 1, 1, 1), (2, 0, 1, 2),
+        (5, 0, 1, 0, 0), (4, 0, 0, 1), (5, 0, 1, 1, 0), (5, 0, 1, 2, 0), (5, 0, 1, 3, 0), (1, 1, 1, 2), (2, 0, 2, 1), (3, 1, 0),
+        (5, 0, 0, 0, 0), (2, 0, 3, 1), (4, 1, 1, 0), (2, 0, 2, 2), (1, 1, 3, 0), (4, 0, 2, 1), (5, 0, 0, 1, 0), (4, 0, 1, 1),
+        (2, 0, 3, 2), (1, 1, 2, 1), (2, 1, 0, 1), (5, 0, 0, 2, 0), (5, 0, 0, 3, 0), (4, 0, 3, 1), (5, 0, 1, 0, 1), (1, 1, 2, 2),
+        (3, 1, 1), (5, 0, 1, 1, 1), (2, 1, 0, 2), (5, 0, 1, 2, 1), (3, 1, 2), (4, 1, 0, 1), (0, 1, 3), (2, 1, 1, 0),
+        (2, 1, 2, 0), (5, 0, 1, 3, 1), (4, 1, 2, 0), (5, 0, 0, 0, 1), (2, 1, 2, 1), (1, 1, 3, 1), (5, 0, 0, 1, 1), (5, 0, 0, 2, 1),
+        (5, 0, 0, 3, 1), (2, 1, 3, 0), (4, 1, 0, 0), (1, 1, 3, 2), (4, 1, 3, 0), (5, 1, 1, 0, 0), (5, 1, 1, 1, 0), (5, 1, 1, 2, 0),
+        (5, 1, 1, 3, 0), (2, 1, 2, 2), (5, 1, 0, 0, 0), (2, 1, 1, 1), (5, 1, 0, 1, 0), (5, 1, 0, 2, 0), (5, 1, 0, 3, 0), (2, 1, 1, 2),
+        (4, 1, 1, 1), (4, 1, 2, 1), (2, 1, 3, 1), (2, 1, 3, 2), (4, 1, 3, 1), (5, 1, 1, 0, 1), (5, 1, 1, 1, 1), (5, 1, 1, 2, 1),
         (5, 1, 1, 3, 1), (5, 1, 0, 0, 1), (5, 1, 0, 1, 1), (5, 1, 0, 2, 1), (5, 1, 0, 3, 1),
     ],
 }
@@ -190,8 +190,6 @@
     for p in range(len(cuts)):
         src = candidates(c, p)
         send(src, src, k_recv.at[p], c_peer, "core")
-    send(mask_hbm, mask.at[1], m_recv.at[0], c_peer, "mask")
-
     owners = [owner_ref[c * spc + l] for l in range(spc)]
     for p in range(len(cuts)):
         arrive(candidates(co, p), k_recv.at[p])
@@ -368,7 +366,7 @@
                     send(total.at[1, done], part.at[done], p_recv.at[0], c_peer, "part")
 
     steps = (own, z_in, y_in, across, row_step, column_step)
-    first_row = True
+    first_row = mask_unsent = True
     for op, *args in program(spc, nz, len(cuts), parts, radix):
         if op == 4 and first_row:
             first_row = False
@@ -376,6 +374,9 @@
                 load.wait()
             arrive(mask.at[1], m_recv.at[0])
         steps[op](*args)
+        if mask_unsent and (op, *args) == (OWN, 0, min(1, len(cuts) - 1)):
+            mask_unsent = False
+            send(mask_hbm, mask.at[1], m_recv.at[0], c_peer, "mask")
 
     arrive(part, p_recv.at[0])
     low = lax.broadcasted_iota(jnp.int32, (m, m), 1) < wide_lane

time: 48.8 us -> 48.3 us (0.990)
  Pallas kernels: 47.2 us -> 46.7 us
    pallas_call x1, Pallas kernels: 47.2 us -> 46.7 us  [local(): pl.pallas_call(functools.partial(kernel, (spc, nk, nz, rows, n, radix)),...]
where the time goes in v4:
time: 48.3 us; the launch traced here: 47.6 us
  Pallas kernels  46.7 us (97%)
  local copies, waits for them, and re-layouts  0.97 us (2%)
    pallas_call x1, Pallas kernels, local(): pl.pallas_call(functools.partial(kernel, (spc, nk, nz, rows, n, radix)),...  46.7 us
    unnamed x1, local copies, waits for them, and re-layouts  0.97 us

profile of v4, /device:TPU:0, one launch (start us, length us, event | category | flops | bytes accessed | tf_op | source)
XLA Modules:
  0.0 47.6 jit_solution(7182934780852531531)
XLA Ops:
  0.0 46.7 %shard_map.64 = f32[512,512]{1,0:T(8,128)S(1)} custom-call(s32[4]{0:T(128)} %owner_ref.1, f32[4]{0:T(128)} %weight_ref.1, f32[2,512,512]{2,1,0:T(8,128)} %bitcast.3, f32[2,2,64,512]{3,2,1,0:T(8,128)} %kern_hbm.1, bf16[4,512,256]{2,1,0:T(8,128)(2,1)} %constant.4.clone.rowt_hbm, bf16[4,2,256,256]{3,2,1,0:T(8,128)(2,1)} %constant.5.clone.colt_hbm), custom_call_target="tpu_custom_call" | custom-call | tf_op jit(solution)/shard_map/pallas_call | solution.py:413
  46.7 1.0 %copy.8 = f32[1,512,512]{2,1,0:T(8,128)} copy(f32[1,512,512]{2,1,0:T(8,128)S(1)} %bitcast.2) | data formatting | bytes 2097152

commit v5 on v4

--- a/solution.py
+++ b/solution.py
@@ -55,18 +55,18 @@
 OWN, Z_IN, Y_IN, ACROSS, ROWS, COLUMNS = range(6)
 TUNED = {
     (2, 4, 4, 3, 4): [
-        (0, 0, 0), (0, 0, 1), (0, 0, 2), (1, 0, 1, 0), (1, 0, 1, 1), (0, 1, 0), (1, 0, 2, 0), (1, 0, 1, 2),
-        (0, 0, 3), (1, 0, 2, 1), (2, 0, 1, 0), (1, 0, 3, 0), (1, 0, 2, 2), (2, 0, 0, 0), (2, 0, 0, 1), (0, 1, 1),
-        (4, 0, 2, 0), (1, 0, 3, 1), (2, 0, 0, 2), (1, 1, 1, 0), (0, 1, 2), (2, 0, 3, 0), (2, 0, 1, 1), (2, 0, 2, 0),
-        (2, 1, 0, 0), (1, 0, 3, 2), (4, 0, 3, 0), (4, 0, 1, 0), (4, 0, 0, 0), (1, 1, 2, 0), (1, 1, 1, 1), (2, 0, 1, 2),
-        (5, 0, 1, 0, 0), (4, 0, 0, 1), (5, 0, 1, 1, 0), (5, 0, 1, 2, 0), (5, 0, 1, 3, 0), (1, 1, 1, 2), (2, 0, 2, 1), (3, 1, 0),
-        (5, 0, 0, 0, 0), (2, 0, 3, 1), (4, 1, 1, 0), (2, 0, 2, 2), (1, 1, 3, 0), (4, 0, 2, 1), (5, 0, 0, 1, 0), (4, 0, 1, 1),
-        (2, 0, 3, 2), (1, 1, 2, 1), (2, 1, 0, 1), (5, 0, 0, 2, 0), (5, 0, 0, 3, 0), (4, 0, 3, 1), (5, 0, 1, 0, 1), (1, 1, 2, 2),
-        (3, 1, 1), (5, 0, 1, 1, 1), (2, 1, 0, 2), (5, 0, 1, 2, 1), (3, 1, 2), (4, 1, 0, 1), (0, 1, 3), (2, 1, 1, 0),
-        (2, 1, 2, 0), (5, 0, 1, 3, 1), (4, 1, 2, 0), (5, 0, 0, 0, 1), (2, 1, 2, 1), (1, 1, 3, 1), (5, 0, 0, 1, 1), (5, 0, 0, 2, 1),
-        (5, 0, 0, 3, 1), (2, 1, 3, 0), (4, 1, 0, 0), (1, 1, 3, 2), (4, 1, 3, 0), (5, 1, 1, 0, 0), (5, 1, 1, 1, 0), (5, 1, 1, 2, 0),
-        (5, 1, 1, 3, 0), (2, 1, 2, 2), (5, 1, 0, 0, 0), (2, 1, 1, 1), (5, 1, 0, 1, 0), (5, 1, 0, 2, 0), (5, 1, 0, 3, 0), (2, 1, 1, 2),
-        (4, 1, 1, 1), (4, 1, 2, 1), (2, 1, 3, 1), (2, 1, 3, 2), (4, 1, 3, 1), (5, 1, 1, 0, 1), (5, 1, 1, 1, 1), (5, 1, 1, 2, 1),
+        (0, 0, 0), (0, 0, 1), (0, 0, 2), (1, 0, 1, 0), (1, 0, 1, 1), (0, 1, 0), (0, 0, 3), (1, 0, 2, 0),
+        (0, 1, 1), (4, 0, 0, 0), (2, 0, 0, 0), (1, 0, 1, 2), (2, 0, 0, 1), (4, 0, 1, 0), (1, 0, 2, 1), (1, 0, 3, 0),
+        (1, 0, 2, 2), (0, 1, 2), (1, 1, 1, 0), (2, 0, 2, 0), (4, 0, 2, 0), (2, 0, 1, 0), (1, 0, 3, 1), (1, 0, 3, 2),
+        (2, 0, 0, 2), (4, 0, 3, 0), (2, 1, 0, 0), (0, 1, 3), (5, 0, 1, 0, 0), (5, 0, 1, 1, 0), (2, 1, 0, 1), (5, 0, 1, 2, 0),
+        (2, 0, 3, 0), (2, 0, 1, 1), (1, 1, 1, 1), (1, 1, 2, 0), (5, 0, 1, 3, 0), (2, 0, 1, 2), (1, 1, 1, 2), (4, 0, 0, 1),
+        (2, 0, 2, 1), (4, 1, 0, 0), (3, 1, 0), (4, 0, 1, 1), (2, 0, 3, 1), (1, 1, 2, 1), (5, 0, 0, 0, 0), (2, 0, 2, 2),
+        (4, 1, 1, 0), (1, 1, 3, 0), (4, 0, 2, 1), (2, 0, 3, 2), (2, 1, 0, 2), (5, 0, 0, 1, 0), (5, 0, 0, 2, 0), (5, 0, 0, 3, 0),
+        (1, 1, 2, 2), (4, 0, 3, 1), (3, 1, 2), (3, 1, 1), (2, 1, 2, 0), (5, 0, 1, 0, 1), (4, 1, 0, 1), (5, 0, 1, 1, 1),
+        (5, 0, 1, 2, 1), (2, 1, 1, 0), (5, 0, 1, 3, 1), (5, 0, 0, 0, 1), (1, 1, 3, 1), (5, 0, 0, 1, 1), (5, 0, 0, 2, 1), (4, 1, 2, 0),
+        (2, 1, 3, 0), (5, 0, 0, 3, 1), (2, 1, 2, 1), (1, 1, 3, 2), (4, 1, 3, 0), (5, 1, 1, 0, 0), (5, 1, 1, 1, 0), (5, 1, 1, 2, 0),
+        (5, 1, 1, 3, 0), (5, 1, 0, 0, 0), (5, 1, 0, 1, 0), (5, 1, 0, 2, 0), (2, 1, 1, 1), (2, 1, 1, 2), (2, 1, 2, 2), (2, 1, 3, 1),
+        (4, 1, 1, 1), (5, 1, 0, 3, 0), (4, 1, 2, 1), (2, 1, 3, 2), (4, 1, 3, 1), (5, 1, 1, 0, 1), (5, 1, 1, 1, 1), (5, 1, 1, 2, 1),
         (5, 1, 1, 3, 1), (5, 1, 0, 0, 1), (5, 1, 0, 1, 1), (5, 1, 0, 2, 1), (5, 1, 0, 3, 1),
     ],
 }
@@ -430,7 +430,7 @@
             pltpu.VMEM((radix, m, n), F32),
             pltpu.VMEM((radix, n, m), F32),
             dma((3 + most,)), dma((most,)), dma((1,)), dma((spc, most + 1)), dma((spc, nz, kept)), dma((spc, nz, kept)),
-            dma((spc, nz, 2)), dma((1,)), dma((4 * nz + 2,)),
+            dma((spc, nz, 2)), dma((1,)), dma((4 * nz - 1,)),
         ] + [pltpu.VMEM((2 * nk, 2, rows // most, n), F32)] * most,
         compiler_params=pltpu.CompilerParams(collective_id=0, has_side_effects=True, vmem_limit_bytes=54 * 1024 * 1024),
     )(owner_table, step_weight, mask_spectrum[0], kernels, jnp.asarray(rowt), jnp.asarray(colt))

time: 48.3 us -> 48.3 us (level)
  no operation moved by 1% of the time
where the time goes in v5:
time: 48.3 us; the launch traced here: 47.6 us
  Pallas kernels  46.6 us (96%)
  local copies, waits for them, and re-layouts  0.97 us (2%)
    pallas_call x1, Pallas kernels, local(): pl.pallas_call(functools.partial(kernel, (spc, nk, nz, rows, n, radix)),...  46.6 us
    unnamed x1, local copies, waits for them, and re-layouts  0.97 us

profile of v5, /device:TPU:0, one launch (start us, length us, event | category | flops | bytes accessed | tf_op | source)
XLA Modules:
  0.0 47.6 jit_solution(7029697785792879907)
XLA Ops:
  0.0 46.6 %shard_map.64 = f32[512,512]{1,0:T(8,128)S(1)} custom-call(s32[4]{0:T(128)} %owner_ref.1, f32[4]{0:T(128)} %weight_ref.1, f32[2,512,512]{2,1,0:T(8,128)} %bitcast.3, f32[2,2,64,512]{3,2,1,0:T(8,128)} %kern_hbm.1, bf16[4,512,256]{2,1,0:T(8,128)(2,1)} %constant.4.clone.rowt_hbm, bf16[4,2,256,256]{3,2,1,0:T(8,128)(2,1)} %constant.5.clone.colt_hbm), custom_call_target="tpu_custom_call" | custom-call | tf_op jit(solution)/shard_map/pallas_call | solution.py:413
  46.6 1.0 %copy.8 = f32[1,512,512]{2,1,0:T(8,128)} copy(f32[1,512,512]{2,1,0:T(8,128)S(1)} %bitcast.2) | data formatting | bytes 2097152
